TPU v7x, 8 devices: a whole 2x2x1 slice. The times are simulated.
8 devices in a mesh: seqs: 2 (over z, y), states: 4 (over x, core).
Axes of the slice: x: 2, y: 2, z: 1, core: 2. Of those that a mesh axis runs over, the one named last changes fastest.
Arguments:
- u_factor: bfloat16 [16384, 1024], P('states')
- w_factor: bfloat16 [16384, 1024], P('states')
- emission: bfloat16 [16384, 10000], P('states')
- init_prob: float32 [16384], P('states')
- tokens: int32 [32, 256], P('seqs'), parts along dimension 0
- lengths: int32 [32], P('seqs'), parts along dimension 0
Outputs:
- output 1: float32 [32], P('seqs'), parts along dimension 0
- output 2: float32 [32, 16384], P('seqs', 'states'), parts along dimension 0
There are 2 independent parts. A program takes and returns all parts, laid end to end along the dimension named above; an argument that names none is the same for every part.
All inputs are finite; a program needn't handle non-finite values.
Results may differ from a plain program's by a relative error of at most 0.001.
Values are sent between devices in bfloat16 or wider.
A program may use at most 1 GiB of HBM per device.

v0:
```python
import jax
import jax.numpy as jnp
from jax import lax
from jax.sharding import PartitionSpec as P


def solution(mesh):
    def local_run(u_own, w_own, emit_own, prob_own, tokens, lengths):
        num_steps = tokens.shape[1]
        emit_first = jnp.take(emit_own, tokens[:, 0], axis=1).T.astype(jnp.float32)
        alpha_init = prob_own[None, :] * emit_first
        norm_init = lax.psum(jnp.sum(alpha_init, axis=1), "states")
        alpha_init = alpha_init / norm_init[:, None]

        def step_body(step_idx, carry):
            alpha_prev, loglik_acc = carry
            z_part = jnp.dot(alpha_prev.astype(jnp.bfloat16), u_own, preferred_element_type=jnp.float32)
            z_feat = lax.psum(z_part, "states")
            mixed_prob = lax.dot_general(z_feat.astype(jnp.bfloat16), w_own, (((1,), (1,)), ((), ())), preferred_element_type=jnp.float32)
            step_tok = lax.dynamic_index_in_dim(tokens, step_idx, axis=1, keepdims=False)
            emit_col = jnp.take(emit_own, step_tok, axis=1).T.astype(jnp.float32)
            alpha_new = mixed_prob * emit_col
            row_norm = lax.psum(jnp.sum(alpha_new, axis=1), "states")
            alpha_new = alpha_new / row_norm[:, None]
            active = step_idx < lengths
            alpha_next = jnp.where(active[:, None], alpha_new, alpha_prev)
            loglik_next = loglik_acc + jnp.where(active, jnp.log(row_norm), 0.0)
            return alpha_next, loglik_next

        alpha_last, loglik = lax.fori_loop(1, num_steps, step_body, (alpha_init, jnp.log(norm_init)))
        return loglik, alpha_last

    return jax.shard_map(
        local_run,
        mesh=mesh,
        in_specs=(P("states", None), P("states", None), P("states", None), P("states"), P("seqs", None), P("seqs")),
        out_specs=(P("seqs"), P("seqs", "states")),
        check_vma=False,
    )
```

profile of v0, /device:TPU:0, one launch (start us, length us, event | category | flops | bytes accessed | tf_op | source)
XLA Modules:
  0.0 7443.3 jit_solution(1999224649663917337)
XLA Ops:
  12.4 7430.2 %while.17 = (s32[]{:T(128)}, f32[16,4096]{1,0:T(8,128)S(1)}, f32[16]{0:T(128)S(1)}, s32[16]{0:T(128)S(1)}, bf16[4096,1024]{1,0:T(8,128)(2,1)}, /*index=5*/bf16[4...) while((s32[]{:T(128)}, f32[16,4096]{1,0:T(8,128)S(1)}, ...), condition=%wide.region_6.8_spmd, body=%wide.region_2.7_spmd.sunk | while | flops 268911744 | bytes 18682840 | solution.py:30
  74.7 11.8 psum.38
  162.4 11.3 psum.38
  278.9 11.3 psum.38
  395.5 11.3 psum.38
  512.0 11.3 psum.38
  628.6 11.3 psum.38
  745.1 11.3 psum.38
  861.6 11.3 psum.38
  978.2 11.3 psum.38
  1094.7 11.3 psum.38
  1211.3 11.3 psum.38
  1327.8 11.3 psum.38
  1560.9 11.3 psum.38
  1677.5 11.3 psum.38
  1794.0 11.3 psum.38
  1910.6 11.3 psum.38
  2027.1 11.3 psum.38
  2143.7 11.3 psum.38
  2260.2 11.3 psum.38
  2376.8 11.3 psum.38
  2493.3 11.3 psum.38
  2726.4 11.3 psum.38
  2842.9 11.3 psum.38
  2959.5 11.3 psum.38
  3076.0 11.3 psum.38
  3192.6 11.3 psum.38
  3309.2 11.3 psum.38
  3425.7 11.3 psum.38
  3542.2 11.3 psum.38
  3658.8 11.3 psum.38
  3775.4 11.3 psum.38
  (2284 shorter events, 7076.6 us)
Async XLA Ops:
  0.6 11.7 copy-start.2
  0.6 2.6 copy-start.1
  0.7 11.8 copy-start.3
  7442.6 0.7 copy-start
  7442.6 0.7 copy-start.4
where the time goes:
time: 7540 us; the launch traced here: 7440 us
  blocking collectives  4330 us (57%)
  matrix products  2640 us (35%)
  local copies, waits for them, and re-layouts  423 us (6%)
    psum x255, blocking collectives, step_body(): z_feat = lax.psum(z_part, 'states')  2830 us
    psum x255, blocking collectives, step_body(): row_norm = lax.psum(jnp.sum(alpha_new, axis=1), 'states')  1490 us
    dot_general x255, matrix products, step_body(): lax.dot_general(z_feat.astype(jnp.bfloat16), w_own, (((1,), (1,)), ((), (...  1470 us
    dot_general x255, matrix products, step_body(): jnp.dot(alpha_prev.astype(jnp.bfloat16), u_own, preferred_element_type=jn...  1170 us
    gather x255, local copies, waits for them, and re-layouts, step_body(): emit_col = jnp.take(emit_own, step_tok, axis=1).T.astype(jnp.float32)  419 us

commit v1 on v0

v1 whole, which is shorter than its diff:
```python
import functools

import jax
import jax.numpy as jnp
from jax import lax
from jax.experimental import pallas as pl
from jax.experimental.pallas import tpu as pltpu
from jax.sharding import PartitionSpec as P

MESH = pl.DeviceIdType.MESH
NC = 4
VR = 4
F32 = jnp.float32


def lane_sums(n):
    acc = n[:, :128]
    for k in range(1, n.shape[1] // 128):
        acc = acc + n[:, k * 128:(k + 1) * 128]
    return acc


def forward_kernel(g_hbm, v_hbm, u_ref, wt_ref, pi_ref, len_ref, ll_ref, alpha_ref,
                   gbuf, nb, mixed, zsend, zrecv, zbuf, cbuf, c0buf, c0recv, vown, vrecv,
                   gsem, zs_far, zs_near, zr, zb_s, zb_r, cs, cr, c0s, c0r, vl, vs_far, vs_near, vr):
    me = lax.axis_index("states")
    seq = lax.axis_index("seqs")
    core = lax.rem(me, 2)
    chip = me // 2
    hub = core == 1
    partner = me + 1 - 2 * core
    far_hub = (1 - chip) * 2 + 1
    src = 1 - core
    num_steps = g_hbm.shape[0]
    ch = zsend.shape[-1]

    def remote(src_ref, dst_ref, ssem, rsem, dev):
        return pltpu.make_async_remote_copy(src_ref=src_ref, dst_ref=dst_ref, send_sem=ssem, recv_sem=rsem,
                                            device_id=(seq, dev), device_id_type=MESH)

    def fetch(t, slot):
        return pltpu.make_async_copy(g_hbm.at[t], gbuf.at[slot], gsem.at[slot])

    def z_far(slot, j, who=src):
        return remote(zsend.at[slot, j], zrecv.at[slot, who, j], zs_far.at[slot, j], zr.at[slot, who, j], far_hub)

    def z_near(slot, j):
        return remote(zsend.at[slot, j], zrecv.at[slot, 2, j], zs_near.at[slot, j], zr.at[slot, 2, j], partner)

    def z_down(slot, j):
        return remote(zbuf.at[slot, j], zbuf.at[slot, j], zb_s.at[slot, j], zb_r.at[slot, j], partner)

    def c_down(slot):
        return remote(cbuf.at[slot], cbuf.at[slot], cs.at[slot], cr.at[slot], partner)

    def v_local(t, s):
        return pltpu.make_async_copy(v_hbm.at[t], vown.at[s], vl.at[s])

    def v_far(t, s, who=src):
        return remote(v_hbm.at[t], vrecv.at[s, who], vs_far.at[s], vr.at[s, who], far_hub)

    def v_near(t, s):
        return remote(v_hbm.at[t], vrecv.at[s, 2], vs_near.at[s], vr.at[s, 2], partner)

    def v_send(t):
        s = lax.rem(t, VR)
        v_local(t, s).start()
        v_far(t, s).start()
        v_near(t, s).start()

    peers = [lax.rem(me + d, 4) for d in range(1, 4)]
    barrier = pltpu.get_barrier_semaphore()
    for q in peers:
        pl.semaphore_signal(barrier, inc=1, device_id=(seq, q), device_id_type=MESH)
    fetch(0, 0).start()
    fetch(1, 1).start()
    pl.semaphore_wait(barrier, 3)
    v_send(1)
    v_send(2)
    fetch(0, 0).wait()
    n0 = pi_ref[...] * gbuf[0].astype(F32)
    c0buf[...] = lane_sums(n0)
    first = [remote(c0buf, c0recv.at[i], c0s.at[i], c0r.at[i], peers[i]) for i in range(3)]
    for cp in first:
        cp.start()
    for cp in first:
        cp.wait()
    c = jnp.sum(c0buf[...] + c0recv[0] + c0recv[1] + c0recv[2], axis=1, keepdims=True)
    a0 = n0 / c
    alpha_ref[...] = a0
    nb[...] = a0.astype(jnp.bfloat16)
    ll_ref[...] = jnp.broadcast_to(jnp.log(c), ll_ref.shape)

    def send(t):
        slot = lax.rem(t, 2)
        for j in range(NC):
            zsend[slot, j] = jnp.dot(nb[...], u_ref[:, j * ch:(j + 1) * ch], preferred_element_type=F32)
            z_far(slot, j).start()
            z_near(slot, j).start()

        @pl.when(t + 2 < num_steps)
        def _():
            v_send(t + 2)

    def receive(t):
        slot = lax.rem(t, 2)
        vslot = lax.rem(t, VR)

        @pl.when(t + 1 < num_steps)
        def _():
            fetch(t + 1, 1 - slot).start()

        v_local(t, vslot).wait()
        v_far(t, vslot).wait_send()
        v_near(t, vslot).wait_send()
        v_near(t, vslot).wait_recv()

        @pl.when(hub)
        def _():
            @pl.when(t > 1)
            def _():
                for j in range(NC):
                    z_down(1 - slot, j).wait_send()
                c_down(1 - slot).wait_send()
            for who in range(2):
                v_far(t, vslot, who).wait_recv()
            cbuf[slot] = jnp.zeros(cbuf.shape[1:], F32)

        for j in range(NC):
            @pl.when(hub)
            def _():
                z_near(slot, j).wait_recv()
                for who in range(2):
                    z_far(slot, j, who).wait_recv()
                z = (zsend[slot, j] + zrecv[slot, 2, j]) + (zrecv[slot, 0, j] + zrecv[slot, 1, j])
                zb = z.astype(jnp.bfloat16)
                zbuf[slot, j] = zb
                z_down(slot, j).start()
                cols = pl.ds(j * ch, ch)
                v = (vown[vslot, :, cols] + vrecv[vslot, 2, :, cols]) + (vrecv[vslot, 0, :, cols] + vrecv[vslot, 1, :, cols])
                cbuf[slot] = cbuf[slot] + lane_sums(zb.astype(F32) * v)
                if j == NC - 1:
                    c_down(slot).start()

            @pl.when(jnp.logical_not(hub))
            def _():
                z_near(slot, j).wait_recv()
                z_down(slot, j).wait_recv()
                if j == NC - 1:
                    c_down(slot).wait_recv()

            if j == NC - 1:
                for i in range(NC):
                    z_far(slot, i).wait_send()
                    z_near(slot, i).wait_send()
                fetch(t, slot).wait()
            part = jnp.dot(zbuf[slot, j], wt_ref[j * ch:(j + 1) * ch, :], preferred_element_type=F32)
            if j == 0:
                mixed[...] = part
            elif j < NC - 1:
                mixed[...] = mixed[...] + part
        u = mixed[...] + part
        c = jnp.sum(cbuf[slot], axis=1, keepdims=True)
        active = t < len_ref[...]
        a = jnp.where(active[:, :1], (u * gbuf[slot].astype(F32)) * (1.0 / c), alpha_ref[...])
        alpha_ref[...] = a
        nb[...] = a.astype(jnp.bfloat16)
        ll_ref[...] = ll_ref[...] + jnp.where(active, jnp.log(c), 0.0)

    send(1)

    def step(t, carry):
        receive(t)
        send(t + 1)
        return carry

    lax.fori_loop(1, num_steps - 1, step, 0)
    receive(num_steps - 1)

    @pl.when(hub)
    def _():
        slot = (num_steps - 1) % 2
        for j in range(NC):
            z_down(slot, j).wait_send()
        c_down(slot).wait_send()


def solution(mesh):
    def local_run(u_own, w_own, emit_own, prob_own, tokens, lengths):
        batch, num_steps = tokens.shape
        states, rank = u_own.shape
        ch = rank // NC
        g = jnp.take(emit_own.T, tokens.T.reshape(-1), axis=0, mode="clip")
        v = jnp.dot(g, w_own, preferred_element_type=F32).reshape(num_steps, batch, rank)
        g = g.reshape(num_steps, batch, states)
        lens = jnp.broadcast_to(lengths[:, None], (batch, 128))
        vm = pl.BlockSpec(memory_space=pltpu.VMEM)
        hbm = pl.BlockSpec(memory_space=pltpu.HBM)
        dma = pltpu.SemaphoreType.DMA
        bf16 = jnp.bfloat16
        ll, alpha = pl.pallas_call(
            forward_kernel,
            out_shape=(jax.ShapeDtypeStruct((batch, 128), F32),
                       jax.ShapeDtypeStruct((batch, states), F32)),
            in_specs=[hbm, hbm, vm, vm, vm, vm],
            out_specs=(vm, vm),
            scratch_shapes=[
                pltpu.VMEM((2, batch, states), bf16),
                pltpu.VMEM((batch, states), bf16),
                pltpu.VMEM((batch, states), F32),
                pltpu.VMEM((2, NC, batch, ch), F32),
                pltpu.VMEM((2, 3, NC, batch, ch), F32),
                pltpu.VMEM((2, NC, batch, ch), bf16),
                pltpu.VMEM((2, batch, 128), F32),
                pltpu.VMEM((batch, 128), F32),
                pltpu.VMEM((3, batch, 128), F32),
                pltpu.VMEM((VR, batch, rank), F32),
                pltpu.VMEM((VR, 3, batch, rank), F32),
                dma((2,)), dma((2, NC)), dma((2, NC)), dma((2, 3, NC)), dma((2, NC)), dma((2, NC)),
                dma((2,)), dma((2,)), dma((3,)), dma((3,)), dma((VR,)), dma((VR,)), dma((VR,)), dma((VR, 3)),
            ],
            compiler_params=pltpu.CompilerParams(
                collective_id=0, has_side_effects=True, vmem_limit_bytes=48 << 20),
            name="hmm_forward",
        )(g, v, u_own, w_own.T, prob_own[None, :], lens)
        return ll[:, 0], alpha

    return jax.shard_map(
        local_run,
        mesh=mesh,
        in_specs=(P("states", None), P("states", None), P("states", None), P("states"), P("seqs", None), P("seqs")),
        out_specs=(P("seqs"), P("seqs", "states")),
        check_vma=False,
    )
```

time: 7540 us -> 1780 us (0.24); the launches traced: 7440 us -> 1770 us
  blocking collectives: 4330 us -> 0 us
  matrix products: 2640 us -> 42.9 us
  Pallas kernels: 0 us -> 1580 us
  local copies, waits for them, and re-layouts: 423 us -> 147 us
    psum x511 -> x0, blocking collectives: 4330 us -> none  [the longest x255 2830 us: step_body(): z_feat = lax.psum(z_part, 'states')]
    dot_general x510 -> x1, matrix products: 2640 us -> 42.9 us  [local_run(): jnp.dot(g, w_own, preferred_element_type=F32)]
    pallas_call x0 -> x1, Pallas kernels: none -> 1580 us  [local_run(): pl.pallas_call(forward_kernel, out_shape=(jax.ShapeDtypeStruct((batch, 12...]
    gather x256 -> x1, local copies, waits for them, and re-layouts: 421 us -> 132 us  [local_run(): g = jnp.take(emit_own.T, tokens.T.reshape(-1), axis=0, mode='clip')]
where the time goes in v1:
time: 1780 us; the launch traced here: 1770 us
  Pallas kernels  1580 us (89%)
  local copies, waits for them, and re-layouts  147 us (8%)
  matrix products  42.9 us (2%)
    pallas_call x1, Pallas kernels, local_run(): pl.pallas_call(forward_kernel, out_shape=(jax.ShapeDtypeStruct((batch, 12...  1580 us
    gather x1, local copies, waits for them, and re-layouts, local_run(): g = jnp.take(emit_own.T, tokens.T.reshape(-1), axis=0, mode='clip')  132 us
    dot_general x1, matrix products, local_run(): jnp.dot(g, w_own, preferred_element_type=F32)  42.9 us

profile of v1, /device:TPU:0, one launch (start us, length us, event | category | flops | bytes accessed | tf_op | source)
XLA Modules:
  0.0 1774.6 jit_solution(9442697969703821001)
XLA Ops:
  0.6 0.7 broadcast_in_dim.15.len_ref
  1.4 0.8 copy.9
  2.2 0.1 reshape.17
  2.3 11.5 copy.10
  13.8 132.5 %gather_fusion = bf16[4096,4096]{1,0:T(8,128)(2,1)} fusion(bf16[10000,4096]{1,0:T(8,128)(2,1)} %bitcast, s32[4096]{0:T(1024)S(1)} %broadcast_clamp_fusion), kind=kCustom, calls=%fused_computation | custom fusion | bytes 67125248 | tf_op jit(solution)/shard_map/jit(_take)/gather | solution.py:193
  146.3 0.0 copy-start
  146.3 42.9 %fusion = f32[4096,1024]{1,0:T(8,128)} fusion(bf16[4096,4096]{1,0:T(8,128)(2,1)} %gather_fusion, bf16[4096,1024]{1,0:T(8,128)(2,1)} %param.7), kind=kOutput, calls=%fused_computation.3 | convolution fusion | flops 34359738368 | bytes 58720256 | tf_op jit(solution)/shard_map/dot_general | solution.py:194
  189.2 0.0 copy-done
  189.2 1584.0 %hmm_forward.1 = (f32[16,128]{1,0:T(8,128)S(1)}, f32[16,4096]{1,0:T(8,128)S(1)}) custom-call(bf16[256,16,4096]{2,1,0:T(8,128)(2,1)} %bitcast.9, f32[256,16,1024]{2,1,0:T(8,128)} %bitcast.11, bf16[4096,1024]{1,0:T(8,128)(2,1)} %u_ref.1, bf16[1024,4096]{1,0:T(8,128)(2,1)} %bitcast.10, f32[1,4096]{1,0:T(1,128)S(1)} %bitcast.8, ...), custom_call_target="tpu_custom_call" | custom-call | tf_op jit(solution)/shard_map/hmm_forward/pallas_call | solution.py:201
  1773.2 0.6 slice_reduce_fusion
  1773.9 0.7 copy.12
  (1 shorter events, 0.0 us)
Async XLA Ops:
  146.3 43.0 %copy-start = (f32[4096]{0:T(1024)S(1)}, f32[4096]{0:T(1024)}, u32[]{:S(2)}) copy-start(f32[4096]{0:T(1024)} %param.9) | copy-start | bytes 49156

commit v2 on v0

v2 whole, which is shorter than its diff:
```python
import jax
import jax.numpy as jnp
from jax import lax
from jax.experimental import pallas as pl
from jax.experimental.pallas import tpu as pltpu
from jax.sharding import PartitionSpec as P

MESH = pl.DeviceIdType.MESH
NC = 4
RING = 4
MOVE = 2048
BLK = 128
F32 = jnp.float32
BF16 = jnp.bfloat16


def lane_sums(n):
    acc = n[:, :128]
    for k in range(1, n.shape[1] // 128):
        acc = acc + n[:, k * 128:(k + 1) * 128]
    return acc


def forward_kernel(g_hbm, v_hbm, u_hbm, wt_hbm, pi_ref, len_ref, ll_ref, alpha_ref,
                   u_ref, wt_ref, a_ref, gbuf, nb, mixed, zsend, zrecv, zbuf, cbuf, c0buf, c0recv, vown, vrecv, vsum,
                   ul, wl, um, wm, am, gl, gm_s, gm_r, zf, zn, zr, zd_s, zd_r, cd_s, cd_r, c0s, c0r, vl, vf, vn, vr):
    me = lax.axis_index("states")
    seq = lax.axis_index("seqs")
    core = lax.rem(me, 2)
    chip = me // 2
    hub = core == 1
    partner = me + 1 - 2 * core
    far_hub = (1 - chip) * 2 + 1
    num_steps, _, own = g_hbm.shape
    keep = own - MOVE
    ch = zsend.shape[-1]

    def remote(src_ref, dst_ref, ssem, rsem, dev):
        return pltpu.make_async_remote_copy(src_ref=src_ref, dst_ref=dst_ref, send_sem=ssem, recv_sem=rsem,
                                            device_id=(seq, dev), device_id_type=MESH)

    kept, moved, added = pl.ds(0, keep), pl.ds(keep, MOVE), pl.ds(own, MOVE)
    u_move = remote(u_hbm.at[moved, :], u_ref.at[added, :], um.at[0], um.at[1], partner)
    w_move = remote(wt_hbm.at[:, moved], wt_ref.at[:, added], wm.at[0], wm.at[1], partner)
    a_move = remote(a_ref.at[:, moved], a_ref.at[:, added], am.at[0], am.at[1], partner)
    a_back = remote(a_ref.at[:, added], a_ref.at[:, moved], am.at[2], am.at[3], partner)
    u_load = pltpu.make_async_copy(u_hbm, u_ref.at[pl.ds(0, own), :], ul)
    w_load = pltpu.make_async_copy(wt_hbm, wt_ref.at[:, pl.ds(0, own)], wl)

    def g_local(t):
        s = lax.rem(t, RING)
        return pltpu.make_async_copy(g_hbm.at[t], gbuf.at[s, :, pl.ds(0, own)], gl.at[s])

    def g_move(t):
        s = lax.rem(t, RING)
        return remote(g_hbm.at[t, :, moved], gbuf.at[s, :, added], gm_s.at[s], gm_r.at[s], partner)

    def z_far(slot, j, who):
        return remote(zsend.at[slot, j], zrecv.at[slot, who, j], zf.at[slot, j], zr.at[slot, who, j], far_hub)

    def z_near(slot, j):
        return remote(zsend.at[slot, j], zrecv.at[slot, 2, j], zn.at[slot, j], zr.at[slot, 2, j], partner)

    def z_down(slot, j):
        return remote(zbuf.at[slot, j], zbuf.at[slot, j], zd_s.at[slot, j], zd_r.at[slot, j], partner)

    def c_down(slot):
        return remote(cbuf.at[slot], cbuf.at[slot], cd_s.at[slot], cd_r.at[slot], partner)

    def v_local(t):
        s = lax.rem(t, RING)
        return pltpu.make_async_copy(v_hbm.at[t], vown.at[s], vl.at[s])

    def v_far(t, who):
        s = lax.rem(t, RING)
        return remote(v_hbm.at[t], vrecv.at[s, who], vf.at[s], vr.at[s, who], far_hub)

    def v_near(t):
        s = lax.rem(t, RING)
        return remote(v_hbm.at[t], vrecv.at[s, 2], vn.at[s], vr.at[s, 2], partner)

    def ahead_hub(t):
        g_local(t).start()
        v_far(t, 0).start()
        v_local(t).start()

    def ahead_even(t):
        g_local(t).start()
        g_move(t).start()
        v_near(t).start()
        v_far(t, 1).start()

    def update(t, u, n_states):
        slot = lax.rem(t, 2)
        c = jnp.sum(cbuf[slot], axis=1, keepdims=True)
        active = t < len_ref[...]
        cols = pl.ds(0, n_states)
        n = u * gbuf[lax.rem(t, RING), :, cols].astype(F32)
        a = jnp.where(active[:, :1], n * (1.0 / c), a_ref[:, cols])
        a_ref[:, cols] = a
        nb[:, cols] = a.astype(BF16)
        ll_ref[...] = ll_ref[...] + jnp.where(active, jnp.log(c), 0.0)

    def dot_w(slot, j, n_states):
        return jnp.dot(zbuf[slot, j], wt_ref[j * ch:(j + 1) * ch, :n_states], preferred_element_type=F32)

    def dot_u(j, n_states):
        return jnp.dot(nb[:, :n_states], u_ref[:n_states, pl.ds(pl.multiple_of(j * ch, ch), ch)], preferred_element_type=F32)

    peers = [lax.rem(me + d, 4) for d in range(1, 4)]
    barrier = pltpu.get_barrier_semaphore()
    for q in peers:
        pl.semaphore_signal(barrier, inc=1, device_id=(seq, q), device_id_type=MESH)
    g_local(0).start()
    u_load.start()
    w_load.start()
    pl.semaphore_wait(barrier, 3)

    @pl.when(jnp.logical_not(hub))
    def _():
        u_move.start()
        w_move.start()

    g_local(0).wait()
    n0 = pi_ref[...] * gbuf[0, :, :own].astype(F32)
    c0buf[...] = lane_sums(n0)
    first = [remote(c0buf, c0recv.at[i], c0s.at[i], c0r.at[i], peers[i]) for i in range(3)]
    for cp in first:
        cp.start()
    for cp in first:
        cp.wait()
    c = jnp.sum(c0buf[...] + c0recv[0] + c0recv[1] + c0recv[2], axis=1, keepdims=True)
    a0 = n0 / c
    a_ref[:, :own] = a0
    nb[:, :own] = a0.astype(BF16)
    ll_ref[...] = jnp.broadcast_to(jnp.log(c), ll_ref.shape)
    u_load.wait()
    w_load.wait()

    @pl.when(hub)
    def _():
        total = own + MOVE
        ahead_hub(1)
        ahead_hub(2)
        u_move.wait_recv()
        w_move.wait_recv()
        a_move.wait_recv()
        nb[:, own:] = a_ref[:, own:].astype(BF16)

        def send(t):
            slot = lax.rem(t, 2)

            def chunk(j, carry):
                zsend[slot, j] = dot_u(j, total)
                z_far(slot, j, 0).start()
                return carry

            lax.fori_loop(0, NC, chunk, 0)

            @pl.when(t + 2 < num_steps)
            def _():
                ahead_hub(t + 2)

        def receive(t):
            slot = lax.rem(t, 2)
            ring = lax.rem(t, RING)

            @pl.when(t > 1)
            def _():
                for j in range(NC):
                    z_down(1 - slot, j).wait_send()
                c_down(1 - slot).wait_send()
            v_local(t).wait()
            v_far(t, 0).wait_send()
            for who in range(2):
                v_far(t, who).wait_recv()
            v_near(t).wait_recv()
            g_local(t).wait()
            g_move(t).wait_recv()
            vsum[...] = (vown[ring] + vrecv[ring, 2]) + (vrecv[ring, 0] + vrecv[ring, 1])
            acc = None
            for j in range(NC):
                z_near(slot, j).wait_recv()
                for who in range(2):
                    z_far(slot, j, who).wait_recv()
                z = (zsend[slot, j] + zrecv[slot, 2, j]) + (zrecv[slot, 0, j] + zrecv[slot, 1, j])
                zb = z.astype(BF16)
                zbuf[slot, j] = zb
                z_down(slot, j).start()
                part = lane_sums(zb.astype(F32) * vsum[:, j * ch:(j + 1) * ch])
                acc = part if acc is None else acc + part
                if j == NC - 1:
                    cbuf[slot] = acc
                    c_down(slot).start()
                    for i in range(NC):
                        z_far(slot, i, 0).wait_send()
                u = dot_w(slot, j, total)
                if j == 0:
                    mixed[...] = u
                elif j < NC - 1:
                    mixed[...] = mixed[...] + u
            update(t, mixed[...] + u, total)

        send(1)

        def step(t, carry):
            receive(t)
            send(t + 1)
            return carry

        lax.fori_loop(1, num_steps - 1, step, 0)
        receive(num_steps - 1)
        slot = (num_steps - 1) % 2
        for j in range(NC):
            z_down(slot, j).wait_send()
        c_down(slot).wait_send()
        a_back.start()
        a_back.wait_send()

    @pl.when(jnp.logical_not(hub))
    def _():
        a_move.start()
        ahead_even(1)
        ahead_even(2)
        u_move.wait_send()
        w_move.wait_send()
        a_move.wait_send()

        def send(t):
            slot = lax.rem(t, 2)

            def chunk(j, carry):
                zsend[slot, j] = dot_u(j, keep)
                z_far(slot, j, 1).start()
                z_near(slot, j).start()
                return carry

            lax.fori_loop(0, NC, chunk, 0)

            @pl.when(t + 2 < num_steps)
            def _():
                ahead_even(t + 2)

        def receive(t):
            slot = lax.rem(t, 2)
            v_near(t).wait_send()
            v_far(t, 1).wait_send()
            g_move(t).wait_send()
            g_local(t).wait()
            for i in range(NC):
                z_far(slot, i, 1).wait_send()
                z_near(slot, i).wait_send()
            for j in range(NC):
                z_down(slot, j).wait_recv()
                if j == NC - 1:
                    c_down(slot).wait_recv()
                u = dot_w(slot, j, keep)
                if j == 0:
                    mixed[:, :keep] = u
                elif j < NC - 1:
                    mixed[:, :keep] = mixed[:, :keep] + u
            update(t, mixed[:, :keep] + u, keep)

        send(1)

        def step(t, carry):
            receive(t)
            send(t + 1)
            return carry

        lax.fori_loop(1, num_steps - 1, step, 0)
        receive(num_steps - 1)
        a_back.wait_recv()

    alpha_ref[...] = a_ref[:, :own]


def gather_kernel(row_ref, pick_ref, e_hbm, w_ref, g_ref, v_ref, buf, sem):
    i = pl.program_id(0)
    n = pl.num_programs(0)
    slot = lax.rem(i, 2)

    def start(blk, to):
        for r in range(BLK):
            row = pl.multiple_of(row_ref[blk * BLK + r], 2)
            pltpu.make_async_copy(e_hbm.at[pl.ds(row, 2), :], buf.at[to, pl.ds(2 * r, 2), :], sem.at[to]).start()

    def wait(which):
        pltpu.make_async_copy(e_hbm.at[pl.ds(0, 2 * BLK), :], buf.at[which], sem.at[which]).wait()

    @pl.when(i == 0)
    def _():
        start(0, 0)
    wait(slot)
    start(lax.rem(i + 1, n), 1 - slot)
    g_ref[...] = jnp.dot(pick_ref[...], buf[slot], preferred_element_type=F32).astype(BF16)
    v_ref[...] = jnp.dot(g_ref[...], w_ref[...], preferred_element_type=F32)

    @pl.when(i == n - 1)
    def _():
        wait(1 - slot)


def gather(tok, e, w):
    n = tok.shape[0]
    states, rank = w.shape
    spot = 2 * (jnp.arange(n) % BLK) + tok % 2
    pick = (spot[:, None] == jnp.arange(2 * BLK)[None, :]).astype(BF16)
    return pl.pallas_call(
        gather_kernel,
        grid_spec=pltpu.PrefetchScalarGridSpec(
            num_scalar_prefetch=1, grid=(n // BLK,),
            in_specs=[pl.BlockSpec((BLK, 2 * BLK), lambda i, t: (i, 0)), pl.BlockSpec(memory_space=pltpu.HBM),
                      pl.BlockSpec((states, rank), lambda i, t: (0, 0), pipeline_mode=pl.Buffered(1))],
            out_specs=[pl.BlockSpec((BLK, states), lambda i, t: (i, 0)), pl.BlockSpec((BLK, rank), lambda i, t: (i, 0))],
            scratch_shapes=[pltpu.VMEM((2, 2 * BLK, states), BF16), pltpu.SemaphoreType.DMA((2,))]),
        out_shape=[jax.ShapeDtypeStruct((n, states), BF16), jax.ShapeDtypeStruct((n, rank), F32)],
        compiler_params=pltpu.CompilerParams(vmem_limit_bytes=56 << 20),
        name="gather_rows",
    )(tok - tok % 2, pick, e, w)


def solution(mesh):
    def local_run(u_own, w_own, emit_own, prob_own, tokens, lengths):
        batch, num_steps = tokens.shape
        states, rank = u_own.shape
        ch = rank // NC
        total = states + MOVE
        g, v = gather(tokens.T.reshape(-1), emit_own.T, w_own)
        v = v.reshape(num_steps, batch, rank)
        g = g.reshape(num_steps, batch, states)
        lens = jnp.broadcast_to(lengths[:, None], (batch, 128))
        vm = pl.BlockSpec(memory_space=pltpu.VMEM)
        hbm = pl.BlockSpec(memory_space=pltpu.HBM)
        dma = pltpu.SemaphoreType.DMA
        ll, alpha = pl.pallas_call(
            forward_kernel,
            out_shape=(jax.ShapeDtypeStruct((batch, 128), F32),
                       jax.ShapeDtypeStruct((batch, states), F32)),
            in_specs=[hbm, hbm, hbm, hbm, vm, vm],
            out_specs=(vm, vm),
            scratch_shapes=[
                pltpu.VMEM((total, rank), BF16),
                pltpu.VMEM((rank, total), BF16),
                pltpu.VMEM((batch, total), F32),
                pltpu.VMEM((RING, batch, total), BF16),
                pltpu.VMEM((batch, total), BF16),
                pltpu.VMEM((batch, total), F32),
                pltpu.VMEM((2, NC, batch, ch), F32),
                pltpu.VMEM((2, 3, NC, batch, ch), F32),
                pltpu.VMEM((2, NC, batch, ch), BF16),
                pltpu.VMEM((2, batch, 128), F32),
                pltpu.VMEM((batch, 128), F32),
                pltpu.VMEM((3, batch, 128), F32),
                pltpu.VMEM((RING, batch, rank), F32),
                pltpu.VMEM((RING, 3, batch, rank), F32),
                pltpu.VMEM((batch, rank), F32),
                dma, dma, dma((2,)), dma((2,)), dma((4,)), dma((RING,)), dma((RING,)), dma((RING,)),
                dma((2, NC)), dma((2, NC)), dma((2, 3, NC)), dma((2, NC)), dma((2, NC)),
                dma((2,)), dma((2,)), dma((3,)), dma((3,)), dma((RING,)), dma((RING,)), dma((RING,)), dma((RING, 3)),
            ],
            compiler_params=pltpu.CompilerParams(
                collective_id=0, has_side_effects=True, vmem_limit_bytes=56 << 20),
            name="hmm_forward",
        )(g, v, u_own, w_own.T, prob_own[None, :], lens)
        return ll[:, 0], alpha

    return jax.shard_map(
        local_run,
        mesh=mesh,
        in_specs=(P("states", None), P("states", None), P("states", None), P("states"), P("seqs", None), P("seqs")),
        out_specs=(P("seqs"), P("seqs", "states")),
        check_vma=False,
    )
```

time: 7540 us -> 1430 us (0.19); the launches traced: 7440 us -> 1430 us
  blocking collectives: 4330 us -> 0 us
  matrix products: 2640 us -> 0 us
  Pallas kernels: 0 us -> 1410 us
  local copies, waits for them, and re-layouts: 423 us -> 16.6 us
    psum x511 -> x0, blocking collectives: 4330 us -> none  [the longest x255 2830 us: step_body(): z_feat = lax.psum(z_part, 'states')]
    dot_general x510 -> x0, matrix products: 2640 us -> none  [the longest x255 1470 us: step_body(): lax.dot_general(z_feat.astype(jnp.bfloat16), w_own, (((1,), (1,)), ((), (...]
    pallas_call x0 -> x2, Pallas kernels: none -> 1410 us  [the longest x1 1330 us: local_run(): pl.pallas_call(forward_kernel, out_shape=(jax.ShapeDtypeStruct((batch, 12...]
    gather x256 -> x0, local copies, waits for them, and re-layouts: 421 us -> none  [the longest x255 419 us: step_body(): emit_col = jnp.take(emit_own, step_tok, axis=1).T.astype(jnp.float32)]
where the time goes in v2:
time: 1430 us
  Pallas kernels  1410 us (99%)
  local copies, waits for them, and re-layouts  16.6 us (1%)
    pallas_call x1, Pallas kernels, local_run(): pl.pallas_call(forward_kernel, out_shape=(jax.ShapeDtypeStruct((batch, 12...  1330 us
    pallas_call x1, Pallas kernels, gather(): pl.pallas_call(gather_kernel, grid_spec=pltpu.PrefetchScalarGridSpec(num_...  77.4 us

profile of v2, /device:TPU:0, one launch (start us, length us, event | category | flops | bytes accessed | tf_op | source)
XLA Modules:
  0.0 1425.1 jit_solution(2856591906537454792)
XLA Ops:
  0.6 0.8 copy.9
  1.4 0.1 reshape.46
  1.6 0.6 fusion.3
  2.2 1.7 fusion.pick_ref
  3.9 77.4 %gather_rows.1 = (bf16[4096,4096]{1,0:T(8,128)(2,1)}, f32[4096,1024]{1,0:T(8,128)}) custom-call(s32[4096]{0:T(1024)} %get-tuple-element.11.row_ref, bf16[4096,256]{1,0:T(8,128)(2,1)} %fusion.pick_ref, bf16[10000,4096]{1,0:T(8,128)(2,1)} %bitcast.1.e_hbm, bf16[4096,1024]{1,0:T(8,128)(2,1)} %w_ref.1), custom_call_target="tpu_custom_call" | custom-call | tf_op jit(solution)/shard_map/gather_rows/pallas_call | solution.py:309
  81.3 0.0 copy-start
  81.3 12.0 copy.10
  93.3 0.0 copy-done
  93.3 0.7 broadcast_in_dim.5.len_ref
  94.0 1328.1 %hmm_forward.1 = (f32[16,128]{1,0:T(8,128)}, f32[16,4096]{1,0:T(8,128)}) custom-call(bf16[256,16,4096]{2,1,0:T(8,128)(2,1)} %bitcast.6, f32[256,16,1024]{2,1,0:T(8,128)} %bitcast.8, bf16[4096,1024]{1,0:T(8,128)(2,1)} %u_hbm.1, bf16[1024,4096]{1,0:T(8,128)(2,1)} %bitcast.7, f32[1,4096]{1,0:T(1,128)} %bitcast.9, s32[16,128]{1,0:T(8,128)} %broadcast_in_dim.5.len_ref), custom_call_target="tpu_custom_call" | custom-call | tf_op jit(solution)/shard_map/hmm_forward/pallas_call | solution.py:336
  1422.1 1.3 slice_reduce_fusion
  1423.4 1.7 copy.12
Async XLA Ops:
  81.3 12.0 copy-start

commit v3 on v2

--- a/solution.py
+++ b/solution.py
@@ -229,13 +229,16 @@
         def send(t):
             slot = lax.rem(t, 2)
 
-            def chunk(j, carry):
-                zsend[slot, j] = dot_u(j, keep)
-                z_far(slot, j, 1).start()
-                z_near(slot, j).start()
+            def pair(i, carry):
+                z = jnp.dot(nb[:, :keep], u_ref[:keep, pl.ds(pl.multiple_of(i * 2 * ch, 2 * ch), 2 * ch)],
+                            preferred_element_type=F32)
+                for h in range(2):
+                    zsend[slot, 2 * i + h] = z[:, h * ch:(h + 1) * ch]
+                    z_far(slot, 2 * i + h, 1).start()
+                    z_near(slot, 2 * i + h).start()
                 return carry
 
-            lax.fori_loop(0, NC, chunk, 0)
+            lax.fori_loop(0, NC // 2, pair, 0)
 
             @pl.when(t + 2 < num_steps)
             def _():

time: 1430 us -> 1470 us (1.028)
  Pallas kernels: 1410 us -> 1450 us
    pallas_call x1, Pallas kernels: 1330 us -> 1370 us  [local_run(): pl.pallas_call(forward_kernel, out_shape=(jax.ShapeDtypeStruct((batch, 12...]
where the time goes in v3:
time: 1470 us
  Pallas kernels  1450 us (99%)
  local copies, waits for them, and re-layouts  16.6 us (1%)
    pallas_call x1, Pallas kernels, local_run(): pl.pallas_call(forward_kernel, out_shape=(jax.ShapeDtypeStruct((batch, 12...  1370 us
    pallas_call x1, Pallas kernels, gather(): pl.pallas_call(gather_kernel, grid_spec=pltpu.PrefetchScalarGridSpec(num_...  77.4 us

profile of v3, /device:TPU:0, one launch (start us, length us, event | category | flops | bytes accessed | tf_op | source)
XLA Modules:
  0.0 1467.5 jit_solution(10465132689330834100)
XLA Ops:
  0.6 0.8 copy.9
  1.4 0.1 reshape.46
  1.6 0.6 fusion.3
  2.2 1.7 fusion.pick_ref
  3.9 77.4 %gather_rows.1 = (bf16[4096,4096]{1,0:T(8,128)(2,1)}, f32[4096,1024]{1,0:T(8,128)}) custom-call(s32[4096]{0:T(1024)} %get-tuple-element.11.row_ref, bf16[4096,256]{1,0:T(8,128)(2,1)} %fusion.pick_ref, bf16[10000,4096]{1,0:T(8,128)(2,1)} %bitcast.1.e_hbm, bf16[4096,1024]{1,0:T(8,128)(2,1)} %w_ref.1), custom_call_target="tpu_custom_call" | custom-call | tf_op jit(solution)/shard_map/gather_rows/pallas_call | solution.py:312
  81.3 0.0 copy-start
  81.3 12.0 copy.10
  93.2 0.0 copy-done
  93.2 0.7 broadcast_in_dim.5.len_ref
  93.9 1370.6 %hmm_forward.1 = (f32[16,128]{1,0:T(8,128)}, f32[16,4096]{1,0:T(8,128)}) custom-call(bf16[256,16,4096]{2,1,0:T(8,128)(2,1)} %bitcast.6, f32[256,16,1024]{2,1,0:T(8,128)} %bitcast.8, bf16[4096,1024]{1,0:T(8,128)(2,1)} %u_hbm.1, bf16[1024,4096]{1,0:T(8,128)(2,1)} %bitcast.7, f32[1,4096]{1,0:T(1,128)} %bitcast.9, s32[16,128]{1,0:T(8,128)} %broadcast_in_dim.5.len_ref), custom_call_target="tpu_custom_call" | custom-call | tf_op jit(solution)/shard_map/hmm_forward/pallas_call | solution.py:339
  1464.5 1.3 slice_reduce_fusion
  1465.9 1.7 copy.12
Async XLA Ops:
  81.3 12.0 copy-start
